TPU v7x, 32 devices: a whole 2x2x4 slice. The times are simulated.
32 devices in a mesh: gz: 2 (over x), gx: 2 (over core), gy: 8 (over z, y).
Axes of the slice: x: 2, y: 2, z: 4, core: 2. Of those that a mesh axis runs over, the one named last changes fastest.
Arguments:
- initial_field: float32 [128, 16, 1024], P('gz', 'gx', 'gy'), may hold values from -36 to 36
- plane_coupling: float32 [128, 16, 1024], P('gz', 'gx', 'gy'), may hold values from 0.06 to 0.24
- line_coupling: float32 [128, 16, 1024], P('gz', 'gx', 'gy'), may hold values from 1000 to 8000
- source: float32 [128, 16, 1024], P('gz', 'gx', 'gy'), may hold values from -4 to 4, as said below
- shift_table: float32 [8], replicated, may hold values from 0.5 to 1
- shift_index: int32 [4], replicated, may hold values from 0 to 7
Outputs:
- heated: float32 [128, 16, 1024], P('gz', 'gx', 'gy')
Inputs may be any that keep to these rules, and one draw needn't show every extreme that they name: `shift_index`: one table row for each half-step. A heat source.
All inputs are finite; a program needn't handle non-finite values.
Results may differ from a plain program's by a relative error of at most 0.0003.
Values sent between devices are 32-bit elements; how exact they have to be, the bound alone decides.
A program may use at most 64 MiB of HBM per device.

v0:
```python
import jax
import jax.numpy as jnp
from jax import lax
from jax.sharding import PartitionSpec as P

HALF = 4


def padded_2(cells, sides, width):
    for axis, dim in sides:
        count = lax.axis_size(axis)
        ends = count - 1
        head = lax.slice_in_dim(cells, 0, width, axis=dim)
        tail = lax.slice_in_dim(cells, cells.shape[dim] - width, cells.shape[dim], axis=dim)
        cells = jnp.concatenate(
            [
                lax.ppermute(tail, axis, [(i, (i + 1) % count) for i in range(ends)]),
                cells,
                lax.ppermute(head, axis, [((i + 1) % count, i) for i in range(ends)]),
            ],
            axis=dim,
        )
    return cells


def lookup(shift_table, table_row):
    table_slots = jnp.arange(shift_table.shape[0], dtype=jnp.int32)
    return jnp.sum(jnp.where(table_slots == table_row, shift_table, jnp.zeros_like(shift_table)))


def from_below(values, stride, fill_value, which_axis):
    filler_shape = list(values.shape)
    filler_shape[which_axis] = stride
    filler = jnp.full(filler_shape, fill_value, values.dtype)
    retained = lax.slice_in_dim(values, 0, values.shape[which_axis] - stride, axis=which_axis)
    return jnp.concatenate([filler, retained], axis=which_axis)


def from_above(values, stride, fill_value, which_axis):
    filler_shape = list(values.shape)
    filler_shape[which_axis] = stride
    filler = jnp.full(filler_shape, fill_value, values.dtype)
    retained = lax.slice_in_dim(values, stride, values.shape[which_axis], axis=which_axis)
    return jnp.concatenate([retained, filler], axis=which_axis)


def local_solve(scaled, forcing):
    lower_band = -scaled
    upper_band = -scaled
    main_band = 1.0 + 2.0 * scaled
    layer_count = scaled.shape[0]
    stride = 1
    while stride < layer_count:
        lower_before = from_below(lower_band, stride, 0.0, 0)
        main_before = from_below(main_band, stride, 1.0, 0)
        upper_before = from_below(upper_band, stride, 0.0, 0)
        forcing_before = from_below(forcing, stride, 0.0, 1)
        lower_after = from_above(lower_band, stride, 0.0, 0)
        main_after = from_above(main_band, stride, 1.0, 0)
        upper_after = from_above(upper_band, stride, 0.0, 0)
        forcing_after = from_above(forcing, stride, 0.0, 1)
        left_factor = -lower_band / main_before
        right_factor = -upper_band / main_after
        main_band = main_band + left_factor * upper_before + right_factor * lower_after
        forcing = forcing + left_factor * forcing_before + right_factor * forcing_after
        lower_band = left_factor * lower_before
        upper_band = right_factor * upper_after
        stride = stride * 2
    return forcing / main_band


def reduced_gathered(first_y, last_y, first_f, last_f, first_g, last_g):
    gathered = (
        lax.all_gather(first_y[None], "gz", axis=0, tiled=True),
        lax.all_gather(last_y[None], "gz", axis=0, tiled=True),
        lax.all_gather(first_f[None], "gz", axis=0, tiled=True),
        lax.all_gather(last_f[None], "gz", axis=0, tiled=True),
        lax.all_gather(first_g[None], "gz", axis=0, tiled=True),
        lax.all_gather(last_g[None], "gz", axis=0, tiled=True),
    )
    zero_plane = jnp.zeros_like(first_y)

    def forward(previous, entries):
        offset, slope_part = previous
        start_y, end_y, start_f, end_f, start_g, end_g = entries
        pivot_value = 1.0 - start_f * slope_part
        constant = (start_y + start_f * offset) / pivot_value
        factor = start_g / pivot_value
        next_offset = end_y + end_f * (offset + slope_part * start_y) / pivot_value
        next_slope = end_g + end_f * slope_part * start_g / pivot_value
        return ((next_offset, next_slope), (offset, slope_part, constant, factor))

    final_state, outcome = lax.scan(forward, (zero_plane, zero_plane), gathered)
    offsets, slopes, constants, factors = outcome

    def backward(later_value, entries):
        constant, factor = entries
        own_value = constant + factor * later_value
        return (own_value, (own_value, later_value))

    final_value, solved = lax.scan(backward, zero_plane, (constants, factors), reverse=True)
    own_values, next_values = solved
    device = lax.axis_index("gz")
    offset = lax.dynamic_index_in_dim(offsets, device, 0, keepdims=False)
    slope_part = lax.dynamic_index_in_dim(slopes, device, 0, keepdims=False)
    own_value = lax.dynamic_index_in_dim(own_values, device, 0, keepdims=False)
    next_value = lax.dynamic_index_in_dim(next_values, device, 0, keepdims=False)
    return (offset + slope_part * own_value, next_value)


def on_device(initial_field, plane_coupling, line_coupling, source, shift_table, shift_index):
    layer_count = initial_field.shape[0]
    layer_index = lax.broadcasted_iota(jnp.int32, initial_field.shape, 0)
    current = initial_field
    for half_step in range(HALF):
        shift_value = lookup(shift_table, shift_index[half_step])
        padded = padded_2(current, (("gx", 1), ("gy", 2)), 1)
        beside_all = (
            padded[:, 2:, 1:-1] + padded[:, :-2, 1:-1] + padded[:, 1:-1, 2:] + padded[:, 1:-1, :-2]
        )
        explicit = current + shift_value * (plane_coupling * (beside_all - 4.0 * current) + source)
        scaled = shift_value * line_coupling
        zero_field = jnp.zeros_like(scaled)
        forcing = jnp.stack(
            [
                explicit,
                jnp.where(layer_index == 0, scaled, zero_field),
                jnp.where(layer_index == layer_count - 1, scaled, zero_field),
            ]
        )
        solved = local_solve(scaled, forcing)
        interior = solved[0]
        from_left = solved[1]
        from_right = solved[2]
        left_value, right_value = reduced_gathered(
            interior[0], interior[-1], from_left[0], from_left[-1], from_right[0], from_right[-1]
        )
        current = interior + left_value * from_left + right_value * from_right
    return current


def solution(mesh):
    in_specs = (
        P("gz", "gx", "gy"),
        P("gz", "gx", "gy"),
        P("gz", "gx", "gy"),
        P("gz", "gx", "gy"),
        P(),
        P(),
    )
    out_specs = P("gz", "gx", "gy")
    return jax.shard_map(
        on_device, mesh=mesh, in_specs=in_specs, out_specs=out_specs, check_vma=False
    )
```

profile of v0, /device:TPU:0, one launch (start us, length us, event | category | flops | bytes accessed | tf_op | source)
XLA Modules:
  0.0 313.0 jit_solution(3405564041479087620)
XLA Ops:
  38.9 5.7 %collective-permute-start.3 = (f32[64,10,1]{2,1,0:T(8,128)}, f32[64,10,1]{2,1,0:T(8,128)}, u32[]{:S(2)}, u32[]{:S(2)}) collective-permute-start(f32[64,10,1]{2,1,0:T(8,128)} %get-tuple-element.1420), channel_id=1, source_target_pairs={{0,1},{1,2},{2,3},{3,4},{4,5},{5,6},{6,7},{8,9},{9,10},{10,11},{11... | collective-permute-start | bytes 7688 | tf_op jit(solution)/shard_map/ppermute | solution.py:17
  46.8 19.2 %collective-permute-done.3 = f32[64,10,1]{2,1,0:T(8,128)} collective-permute-done((f32[64,10,1]{2,1,0:T(8,128)}, f32[64,10,1]{2,1,0:T(8,128)}, u32[]{:S(2)}, u32[]{:S(2)}) %collective-permute-start.3) | collective-permute-done | bytes 2592 | tf_op jit(solution)/shard_map/ppermute | solution.py:17
  75.7 4.4 %all-gather = f32[2,1,8,128]{3,2,1,0:T(8,128)S(1)} all-gather(f32[1,1,8,128]{3,2,1,0:T(8,128)S(1)} %get-tuple-element.1400), channel_id=2, replica_groups=mesh['gz'=2,'gx'=2,'gy'=8] {'gz'}, dimensions={0}, use_global_device_ids=true | all-gather | bytes 12288 | tf_op jit(solution)/shard_map/all_gather | solution.py:75
  80.1 4.3 %all-gather.1 = f32[2,1,8,128]{3,2,1,0:T(8,128)S(1)} all-gather(f32[1,1,8,128]{3,2,1,0:T(8,128)S(1)} %get-tuple-element.1399), channel_id=3, replica_groups=mesh['gz'=2,'gx'=2,'gy'=8] {'gz'}, dimensions={0}, use_global_device_ids=true | all-gather | bytes 12288 | tf_op jit(solution)/shard_map/all_gather | solution.py:77
  84.4 4.3 %all-gather.2 = f32[2,1,8,128]{3,2,1,0:T(8,128)S(1)} all-gather(f32[1,1,8,128]{3,2,1,0:T(8,128)S(1)} %get-tuple-element.1398), channel_id=4, replica_groups=mesh['gz'=2,'gx'=2,'gy'=8] {'gz'}, dimensions={0}, use_global_device_ids=true | all-gather | bytes 12288 | tf_op jit(solution)/shard_map/all_gather | solution.py:74
  88.8 4.3 %all-gather.3 = f32[2,1,8,128]{3,2,1,0:T(8,128)S(1)} all-gather(f32[1,1,8,128]{3,2,1,0:T(8,128)S(1)} %get-tuple-element.1397), channel_id=5, replica_groups=mesh['gz'=2,'gx'=2,'gy'=8] {'gz'}, dimensions={0}, use_global_device_ids=true | all-gather | bytes 12288 | tf_op jit(solution)/shard_map/all_gather | solution.py:76
  93.1 4.3 %all-gather.4 = f32[2,1,8,128]{3,2,1,0:T(8,128)S(1)} all-gather(f32[1,1,8,128]{3,2,1,0:T(8,128)S(1)} %get-tuple-element.1396), channel_id=6, replica_groups=mesh['gz'=2,'gx'=2,'gy'=8] {'gz'}, dimensions={0}, use_global_device_ids=true | all-gather | bytes 12288 | tf_op jit(solution)/shard_map/all_gather | solution.py:79
  108.9 4.4 %collective-permute-start.7 = (f32[64,10,1]{2,1,0:T(8,128)}, f32[64,10,1]{2,1,0:T(8,128)S(1)}, u32[]{:S(2)}, u32[]{:S(2)}) collective-permute-start(f32[64,10,1]{2,1,0:T(8,128)} %get-tuple-element.1418), channel_id=1, source_target_pairs={{0,1},{1,2},{2,3},{3,4},{4,5},{5,6},{6,7},{8,9},{9,10},{10,11},{11... | collective-permute-start | bytes 7688 | tf_op jit(solution)/shard_map/ppermute | solution.py:17
  115.5 20.9 %collective-permute-done.7 = f32[64,10,1]{2,1,0:T(8,128)S(1)} collective-permute-done((f32[64,10,1]{2,1,0:T(8,128)}, f32[64,10,1]{2,1,0:T(8,128)S(1)}, u32[]{:S(2)}, u32[]{:S(2)}) %collective-permute-start.7) | collective-permute-done | bytes 2592 | tf_op jit(solution)/shard_map/ppermute | solution.py:17
  145.8 4.4 %all-gather.6 = f32[2,1,8,128]{3,2,1,0:T(8,128)S(1)} all-gather(f32[1,1,8,128]{3,2,1,0:T(8,128)S(1)} %get-tuple-element.1382), channel_id=8, replica_groups=mesh['gz'=2,'gx'=2,'gy'=8] {'gz'}, dimensions={0}, use_global_device_ids=true | all-gather | bytes 12288 | tf_op jit(solution)/shard_map/all_gather | solution.py:75
  150.1 4.3 %all-gather.7 = f32[2,1,8,128]{3,2,1,0:T(8,128)S(1)} all-gather(f32[1,1,8,128]{3,2,1,0:T(8,128)S(1)} %get-tuple-element.1381), channel_id=9, replica_groups=mesh['gz'=2,'gx'=2,'gy'=8] {'gz'}, dimensions={0}, use_global_device_ids=true | all-gather | bytes 12288 | tf_op jit(solution)/shard_map/all_gather | solution.py:77
  163.2 4.3 %all-gather.10 = f32[2,1,8,128]{3,2,1,0:T(8,128)S(1)} all-gather(f32[1,1,8,128]{3,2,1,0:T(8,128)S(1)} %get-tuple-element.1378), channel_id=12, replica_groups=mesh['gz'=2,'gx'=2,'gy'=8] {'gz'}, dimensions={0}, use_global_device_ids=true | all-gather | bytes 12288 | tf_op jit(solution)/shard_map/all_gather | solution.py:79
  167.5 4.3 %all-gather.11 = f32[2,1,8,128]{3,2,1,0:T(8,128)S(1)} all-gather(f32[1,1,8,128]{3,2,1,0:T(8,128)S(1)} %get-tuple-element.1377), channel_id=13, replica_groups=mesh['gz'=2,'gx'=2,'gy'=8] {'gz'}, dimensions={0}, use_global_device_ids=true | all-gather | bytes 12288 | tf_op jit(solution)/shard_map/all_gather | solution.py:78
  178.8 5.1 %collective-permute-start.11 = (f32[64,10,1]{2,1,0:T(8,128)}, f32[64,10,1]{2,1,0:T(8,128)}, u32[]{:S(2)}, u32[]{:S(2)}) collective-permute-start(f32[64,10,1]{2,1,0:T(8,128)} %get-tuple-element.1416), channel_id=1, source_target_pairs={{0,1},{1,2},{2,3},{3,4},{4,5},{5,6},{6,7},{8,9},{9,10},{10,11},{11... | collective-permute-start | bytes 7688 | tf_op jit(solution)/shard_map/ppermute | solution.py:17
  186.0 20.4 %collective-permute-done.11 = f32[64,10,1]{2,1,0:T(8,128)} collective-permute-done((f32[64,10,1]{2,1,0:T(8,128)}, f32[64,10,1]{2,1,0:T(8,128)}, u32[]{:S(2)}, u32[]{:S(2)}) %collective-permute-start.11) | collective-permute-done | bytes 2592 | tf_op jit(solution)/shard_map/ppermute | solution.py:17
  215.9 4.4 %all-gather.12 = f32[2,1,8,128]{3,2,1,0:T(8,128)S(1)} all-gather(f32[1,1,8,128]{3,2,1,0:T(8,128)S(1)} %get-tuple-element.1364), channel_id=14, replica_groups=mesh['gz'=2,'gx'=2,'gy'=8] {'gz'}, dimensions={0}, use_global_device_ids=true | all-gather | bytes 12288 | tf_op jit(solution)/shard_map/all_gather | solution.py:75
  220.3 4.3 %all-gather.13 = f32[2,1,8,128]{3,2,1,0:T(8,128)S(1)} all-gather(f32[1,1,8,128]{3,2,1,0:T(8,128)S(1)} %get-tuple-element.1363), channel_id=15, replica_groups=mesh['gz'=2,'gx'=2,'gy'=8] {'gz'}, dimensions={0}, use_global_device_ids=true | all-gather | bytes 12288 | tf_op jit(solution)/shard_map/all_gather | solution.py:77
  233.3 4.3 %all-gather.16 = f32[2,1,8,128]{3,2,1,0:T(8,128)S(1)} all-gather(f32[1,1,8,128]{3,2,1,0:T(8,128)S(1)} %get-tuple-element.1360), channel_id=18, replica_groups=mesh['gz'=2,'gx'=2,'gy'=8] {'gz'}, dimensions={0}, use_global_device_ids=true | all-gather | bytes 12288 | tf_op jit(solution)/shard_map/all_gather | solution.py:79
  237.7 4.3 %all-gather.17 = f32[2,1,8,128]{3,2,1,0:T(8,128)S(1)} all-gather(f32[1,1,8,128]{3,2,1,0:T(8,128)S(1)} %get-tuple-element.1359), channel_id=19, replica_groups=mesh['gz'=2,'gx'=2,'gy'=8] {'gz'}, dimensions={0}, use_global_device_ids=true | all-gather | bytes 12288 | tf_op jit(solution)/shard_map/all_gather | solution.py:78
  249.2 4.4 %collective-permute-start.15 = (f32[64,10,1]{2,1,0:T(8,128)}, f32[64,10,1]{2,1,0:T(8,128)S(1)}, u32[]{:S(2)}, u32[]{:S(2)}) collective-permute-start(f32[64,10,1]{2,1,0:T(8,128)} %get-tuple-element.1414), channel_id=1, source_target_pairs={{0,1},{1,2},{2,3},{3,4},{4,5},{5,6},{6,7},{8,9},{9,10},{10,11},{11... | collective-permute-start | bytes 7688 | tf_op jit(solution)/shard_map/ppermute | solution.py:17
  255.7 20.9 %collective-permute-done.15 = f32[64,10,1]{2,1,0:T(8,128)S(1)} collective-permute-done((f32[64,10,1]{2,1,0:T(8,128)}, f32[64,10,1]{2,1,0:T(8,128)S(1)}, u32[]{:S(2)}, u32[]{:S(2)}) %collective-permute-start.15) | collective-permute-done | bytes 2592 | tf_op jit(solution)/shard_map/ppermute | solution.py:17
  285.9 4.4 %all-gather.18 = f32[2,1,8,128]{3,2,1,0:T(8,128)S(1)} all-gather(f32[1,1,8,128]{3,2,1,0:T(8,128)S(1)} %get-tuple-element.1346), channel_id=20, replica_groups=mesh['gz'=2,'gx'=2,'gy'=8] {'gz'}, dimensions={0}, use_global_device_ids=true | all-gather | bytes 12288 | tf_op jit(solution)/shard_map/all_gather | solution.py:75
  290.2 4.3 %all-gather.19 = f32[2,1,8,128]{3,2,1,0:T(8,128)S(1)} all-gather(f32[1,1,8,128]{3,2,1,0:T(8,128)S(1)} %get-tuple-element.1345), channel_id=21, replica_groups=mesh['gz'=2,'gx'=2,'gy'=8] {'gz'}, dimensions={0}, use_global_device_ids=true | all-gather | bytes 12288 | tf_op jit(solution)/shard_map/all_gather | solution.py:77
  307.6 4.3 %all-gather.23 = f32[2,1,8,128]{3,2,1,0:T(8,128)S(1)} all-gather(f32[1,1,8,128]{3,2,1,0:T(8,128)S(1)} %get-tuple-element.1341), channel_id=25, replica_groups=mesh['gz'=2,'gx'=2,'gy'=8] {'gz'}, dimensions={0}, use_global_device_ids=true | all-gather | bytes 12288 | tf_op jit(solution)/shard_map/all_gather | solution.py:78
  (511 shorter events, 140.5 us)
Async XLA Ops:
  1.1 36.3 %collective-permute-start = (f32[64,1,128]{2,1,0:T(1,128)S(1)}, f32[64,1,128]{2,1,0:T(1,128)S(1)}, u32[]{:S(2)}, u32[]{:S(2)}) collective-permute-start(f32[64,1,128]{2,1,0:T(1,128)S(1)} %get-tuple-element.1582), channel_id=1, source_target_pairs={{8,0},{9,1},{10,2},{11,3},{12,4},{13,5},{14,6},{15,7},{24,16},{25,... | collective-permute-start | bytes 98312 | tf_op jit(solution)/shard_map/ppermute | solution.py:19
  2.4 35.0 %collective-permute-start.1 = (f32[64,1,128]{2,1,0:T(1,128)S(1)}, f32[64,1,128]{2,1,0:T(1,128)S(1)}, u32[]{:S(2)}, u32[]{:S(2)}) collective-permute-start(f32[64,1,128]{2,1,0:T(1,128)S(1)} %get-tuple-element.1581), channel_id=1, source_target_pairs={{0,8},{1,9},{2,10},{3,11},{4,12},{5,13},{6,14},{7,15},{16,24},{17,... | collective-permute-start | bytes 98312 | tf_op jit(solution)/shard_map/ppermute | solution.py:17
  16.4 51.9 %copy-start.29 = (f32[1,64,8,128]{3,2,1,0:T(8,128)}, f32[1,64,8,128]{3,2,1,0:T(8,128)S(1)}, u32[]{:S(2)}) copy-start(f32[1,64,8,128]{3,2,1,0:T(8,128)S(1)} %get-tuple-element.1468) | copy-start | bytes 786436
  38.9 27.2 %collective-permute-start.3 = (f32[64,10,1]{2,1,0:T(8,128)}, f32[64,10,1]{2,1,0:T(8,128)}, u32[]{:S(2)}, u32[]{:S(2)}) collective-permute-start(f32[64,10,1]{2,1,0:T(8,128)} %get-tuple-element.1420), channel_id=1, source_target_pairs={{0,1},{1,2},{2,3},{3,4},{4,5},{5,6},{6,7},{8,9},{9,10},{10,11},{11... | collective-permute-start | bytes 7688 | tf_op jit(solution)/shard_map/ppermute | solution.py:17
  44.6 21.5 %copy-start = (f32[64,8,128]{2,1,0:T(8,128)S(1)}, f32[64,8,128]{2,1,0:T(8,128)}, u32[]{:S(2)}) copy-start(f32[64,8,128]{2,1,0:T(8,128)} %param.25) | copy-start | bytes 786436
  44.6 21.5 %copy-start.1 = (f32[64,8,128]{2,1,0:T(8,128)S(1)}, f32[64,8,128]{2,1,0:T(8,128)}, u32[]{:S(2)}) copy-start(f32[64,8,128]{2,1,0:T(8,128)} %param.23) | copy-start | bytes 786436
  44.6 21.5 %collective-permute-start.2 = (f32[64,10,1]{2,1,0:T(8,128)}, f32[64,10,1]{2,1,0:T(8,128)}, u32[]{:S(2)}, u32[]{:S(2)}) collective-permute-start(f32[64,10,1]{2,1,0:T(8,128)} %get-tuple-element.1419), channel_id=1, source_target_pairs={{1,0},{2,1},{3,2},{4,3},{5,4},{6,5},{7,6},{9,8},{10,9},{11,10},{12... | collective-permute-start | bytes 7688 | tf_op jit(solution)/shard_map/ppermute | solution.py:19
  102.2 5.4 %collective-permute-start.4 = (f32[64,1,128]{2,1,0:T(1,128)S(1)}, f32[64,1,128]{2,1,0:T(1,128)S(1)}, u32[]{:S(2)}, u32[]{:S(2)}) collective-permute-start(f32[64,1,128]{2,1,0:T(1,128)S(1)} %get-tuple-element.1550), channel_id=1, source_target_pairs={{8,0},{9,1},{10,2},{11,3},{12,4},{13,5},{14,6},{15,7},{24,16},{25,... | collective-permute-start | bytes 98312 | tf_op jit(solution)/shard_map/ppermute | solution.py:19
  103.7 3.9 %collective-permute-start.5 = (f32[64,1,128]{2,1,0:T(1,128)S(1)}, f32[64,1,128]{2,1,0:T(1,128)S(1)}, u32[]{:S(2)}, u32[]{:S(2)}) collective-permute-start(f32[64,1,128]{2,1,0:T(1,128)S(1)} %get-tuple-element.1549), channel_id=1, source_target_pairs={{0,8},{1,9},{2,10},{3,11},{4,12},{5,13},{6,14},{7,15},{16,24},{17,... | collective-permute-start | bytes 98312 | tf_op jit(solution)/shard_map/ppermute | solution.py:17
  108.9 27.6 %collective-permute-start.7 = (f32[64,10,1]{2,1,0:T(8,128)}, f32[64,10,1]{2,1,0:T(8,128)S(1)}, u32[]{:S(2)}, u32[]{:S(2)}) collective-permute-start(f32[64,10,1]{2,1,0:T(8,128)} %get-tuple-element.1418), channel_id=1, source_target_pairs={{0,1},{1,2},{2,3},{3,4},{4,5},{5,6},{6,7},{8,9},{9,10},{10,11},{11... | collective-permute-start | bytes 7688 | tf_op jit(solution)/shard_map/ppermute | solution.py:17
  113.3 23.1 %collective-permute-start.6 = (f32[64,10,1]{2,1,0:T(8,128)}, f32[64,10,1]{2,1,0:T(8,128)}, u32[]{:S(2)}, u32[]{:S(2)}) collective-permute-start(f32[64,10,1]{2,1,0:T(8,128)} %get-tuple-element.1417), channel_id=1, source_target_pairs={{1,0},{2,1},{3,2},{4,3},{5,4},{6,5},{7,6},{9,8},{10,9},{11,10},{12... | collective-permute-start | bytes 7688 | tf_op jit(solution)/shard_map/ppermute | solution.py:19
  115.5 22.9 %copy-start.11 = (f32[1,64,8,128]{3,2,1,0:T(8,128)S(1)}, f32[1,64,8,128]{3,2,1,0:T(8,128)}, u32[]{:S(2)}) copy-start(f32[1,64,8,128]{3,2,1,0:T(8,128)} %get-tuple-element.1463) | copy-start | bytes 786436
  115.5 22.9 %copy-start.12 = (f32[1,64,8,128]{3,2,1,0:T(8,128)S(1)}, f32[1,64,8,128]{3,2,1,0:T(8,128)}, u32[]{:S(2)}) copy-start(f32[1,64,8,128]{3,2,1,0:T(8,128)} %get-tuple-element.1467) | copy-start | bytes 786436
  172.3 5.2 %collective-permute-start.8 = (f32[64,1,128]{2,1,0:T(1,128)S(1)}, f32[64,1,128]{2,1,0:T(1,128)S(1)}, u32[]{:S(2)}, u32[]{:S(2)}) collective-permute-start(f32[64,1,128]{2,1,0:T(1,128)S(1)} %get-tuple-element.1518), channel_id=1, source_target_pairs={{8,0},{9,1},{10,2},{11,3},{12,4},{13,5},{14,6},{15,7},{24,16},{25,... | collective-permute-start | bytes 98312 | tf_op jit(solution)/shard_map/ppermute | solution.py:19
  173.7 3.9 %collective-permute-start.9 = (f32[64,1,128]{2,1,0:T(1,128)S(1)}, f32[64,1,128]{2,1,0:T(1,128)S(1)}, u32[]{:S(2)}, u32[]{:S(2)}) collective-permute-start(f32[64,1,128]{2,1,0:T(1,128)S(1)} %get-tuple-element.1517), channel_id=1, source_target_pairs={{0,8},{1,9},{2,10},{3,11},{4,12},{5,13},{6,14},{7,15},{16,24},{17,... | collective-permute-start | bytes 98312 | tf_op jit(solution)/shard_map/ppermute | solution.py:17
  177.5 7.7 %copy-start.53 = (f32[64,8,128]{2,1,0:T(8,128)}, f32[64,8,128]{2,1,0:T(8,128)S(1)}, u32[]{:S(2)}) copy-start(f32[64,8,128]{2,1,0:T(8,128)S(1)} %get-tuple-element.1221) | copy-start | bytes 786436
  177.7 7.5 %copy-start.43 = (f32[64,8,128]{2,1,0:T(8,128)S(1)}, f32[64,8,128]{2,1,0:T(8,128)}, u32[]{:S(2)}) copy-start(f32[64,8,128]{2,1,0:T(8,128)} %get-tuple-element.1223) | copy-start | bytes 786436
  177.7 7.5 %copy-start.97 = (f32[48,8,128]{2,1,0:T(8,128)S(1)}, f32[48,8,128]{2,1,0:T(8,128)}, u32[]{:S(2)}) copy-start(f32[48,8,128]{2,1,0:T(8,128)} %get-tuple-element.1431) | copy-start | bytes 589828
  178.8 27.5 %collective-permute-start.11 = (f32[64,10,1]{2,1,0:T(8,128)}, f32[64,10,1]{2,1,0:T(8,128)}, u32[]{:S(2)}, u32[]{:S(2)}) collective-permute-start(f32[64,10,1]{2,1,0:T(8,128)} %get-tuple-element.1416), channel_id=1, source_target_pairs={{0,1},{1,2},{2,3},{3,4},{4,5},{5,6},{6,7},{8,9},{9,10},{10,11},{11... | collective-permute-start | bytes 7688 | tf_op jit(solution)/shard_map/ppermute | solution.py:17
  183.9 22.5 %collective-permute-start.10 = (f32[64,10,1]{2,1,0:T(8,128)}, f32[64,10,1]{2,1,0:T(8,128)}, u32[]{:S(2)}, u32[]{:S(2)}) collective-permute-start(f32[64,10,1]{2,1,0:T(8,128)} %get-tuple-element.1415), channel_id=1, source_target_pairs={{1,0},{2,1},{3,2},{4,3},{5,4},{6,5},{7,6},{9,8},{10,9},{11,10},{12... | collective-permute-start | bytes 7688 | tf_op jit(solution)/shard_map/ppermute | solution.py:19
  242.4 5.5 %collective-permute-start.12 = (f32[64,1,128]{2,1,0:T(1,128)S(1)}, f32[64,1,128]{2,1,0:T(1,128)S(1)}, u32[]{:S(2)}, u32[]{:S(2)}) collective-permute-start(f32[64,1,128]{2,1,0:T(1,128)S(1)} %get-tuple-element.1476), channel_id=1, source_target_pairs={{8,0},{9,1},{10,2},{11,3},{12,4},{13,5},{14,6},{15,7},{24,16},{25,... | collective-permute-start | bytes 98312 | tf_op jit(solution)/shard_map/ppermute | solution.py:19
  243.7 4.2 %collective-permute-start.13 = (f32[64,1,128]{2,1,0:T(1,128)S(1)}, f32[64,1,128]{2,1,0:T(1,128)S(1)}, u32[]{:S(2)}, u32[]{:S(2)}) collective-permute-start(f32[64,1,128]{2,1,0:T(1,128)S(1)} %get-tuple-element.1475), channel_id=1, source_target_pairs={{0,8},{1,9},{2,10},{3,11},{4,12},{5,13},{6,14},{7,15},{16,24},{17,... | collective-permute-start | bytes 98312 | tf_op jit(solution)/shard_map/ppermute | solution.py:17
  249.2 27.4 %collective-permute-start.15 = (f32[64,10,1]{2,1,0:T(8,128)}, f32[64,10,1]{2,1,0:T(8,128)S(1)}, u32[]{:S(2)}, u32[]{:S(2)}) collective-permute-start(f32[64,10,1]{2,1,0:T(8,128)} %get-tuple-element.1414), channel_id=1, source_target_pairs={{0,1},{1,2},{2,3},{3,4},{4,5},{5,6},{6,7},{8,9},{9,10},{10,11},{11... | collective-permute-start | bytes 7688 | tf_op jit(solution)/shard_map/ppermute | solution.py:17
  253.6 23.0 %collective-permute-start.14 = (f32[64,10,1]{2,1,0:T(8,128)}, f32[64,10,1]{2,1,0:T(8,128)}, u32[]{:S(2)}, u32[]{:S(2)}) collective-permute-start(f32[64,10,1]{2,1,0:T(8,128)} %get-tuple-element.1413), channel_id=1, source_target_pairs={{1,0},{2,1},{3,2},{4,3},{5,4},{6,5},{7,6},{9,8},{10,9},{11,10},{12... | collective-permute-start | bytes 7688 | tf_op jit(solution)/shard_map/ppermute | solution.py:19
  (93 other events, 116.7 us)
where the time goes:
time: 318 us; the launch traced here: 313 us
  blocking collectives  104 us (33%)
  waiting for transfers between devices  81.5 us (26%)
  local copies, waits for them, and re-layouts  46.7 us (15%)
  starting transfers between devices  42.7 us (13%)
  other arithmetic  34.9 us (11%)
    ppermute x8, waiting for transfers between devices, padded_2(): lax.ppermute(tail, axis, [(i, (i + 1) % count) for i in range(ends)])  81.5 us
    unnamed x202, local copies, waits for them, and re-layouts  33.8 us
    ppermute x8, starting transfers between devices, padded_2(): lax.ppermute(tail, axis, [(i, (i + 1) % count) for i in range(ends)])  31.8 us
    all_gather x4, blocking collectives, reduced_gathered(): lax.all_gather(last_y[None], 'gz', axis=0, tiled=True)  17.4 us
    all_gather x4, blocking collectives, reduced_gathered(): lax.all_gather(last_f[None], 'gz', axis=0, tiled=True)  17.4 us
    all_gather x4, blocking collectives, reduced_gathered(): lax.all_gather(last_g[None], 'gz', axis=0, tiled=True)  17.4 us
    all_gather x4, blocking collectives, reduced_gathered(): lax.all_gather(first_g[None], 'gz', axis=0, tiled=True)  17.4 us
    all_gather x4, blocking collectives, reduced_gathered(): lax.all_gather(first_y[None], 'gz', axis=0, tiled=True)  17.4 us
  transfers between devices with their start and end apart: 16, of which 5 were waited for; matrix products, arithmetic and copies ran while one was open for 8% of the time, Pallas kernels for 0%

commit v1 on v0

v1 whole, which is shorter than its diff:
```python
import functools

import jax
import jax.numpy as jnp
from jax import lax
from jax.experimental import pallas as pl
from jax.experimental.pallas import tpu as pltpu
from jax.sharding import PartitionSpec as P


def loop(count, body, init, unroll, reverse=False):
    while count % unroll:
        unroll -= 1

    def block(i, carry):
        for j in range(unroll):
            k = i * unroll + j
            carry = body(count - 1 - k if reverse else k, carry)
        return carry

    return lax.fori_loop(0, count // unroll, block, init)


def kernel(
    ny_parts, half,
    u_in, pc_in, lc_in, src_in, table, index,
    out,
    u_x, pc_x, lc_x, src_x, to_left, to_right, from_left, from_right,
    p_s, pr_s, b_s, f_s, iq_s, beta_s, beta_r, face_s, face_r,
    in_sem, xs_sem, xr_sem, ys_sem, yr_sem, bs_sem, br_sem, fs_sem, fr_sem,
):
    n, rows, lanes = u_in.shape
    width = half
    per = lanes // width
    groups = n // per
    gz, gx, gy = lax.axis_index("gz"), lax.axis_index("gx"), lax.axis_index("gy")
    has_left, has_right = gy > 0, gy < ny_parts - 1
    own_r, own_c = pl.ds(0, rows), pl.ds(0, lanes)
    other_r, halo_c = pl.ds(rows, rows), pl.ds(lanes, lanes)
    all_r = pl.ds(0, 2 * rows)
    ins = (u_in, pc_in, lc_in, src_in)
    exts = (u_x, pc_x, lc_x, src_x)

    loads = [
        pltpu.make_async_copy(i, e.at[:, own_r, own_c], in_sem.at[a])
        for a, (i, e) in enumerate(zip(ins, exts))
    ]
    for c in loads:
        c.start()

    barrier = pltpu.get_barrier_semaphore()

    def greet(device):
        pl.semaphore_signal(
            barrier, inc=1, device_id=device, device_id_type=pl.DeviceIdType.MESH
        )

    x_peer = (gz, 1 - gx, gy)
    z_peer = (1 - gz, gx, gy)
    left = ((gz, gx, gy - 1), (gz, 1 - gx, gy - 1))
    right = ((gz, gx, gy + 1), (gz, 1 - gx, gy + 1))
    greet(x_peer)
    greet(z_peer)

    @pl.when(has_left)
    def _():
        greet(left[0])
        greet(left[1])

    @pl.when(has_right)
    def _():
        greet(right[0])
        greet(right[1])

    for c in loads:
        c.wait()

    lane = lax.broadcasted_iota(jnp.int32, (rows, lanes), 1)

    def slot(j):
        return (lane >= j * width) & (lane < j * width + width)

    def pack(j, carry):
        at_right = slot(j)
        at_left = slot((j + 1) % per)
        done = []
        for i, (e, g) in enumerate((e, g) for e in exts for g in range(groups)):
            t = pltpu.roll(e[g * per + j, own_r, own_c], ((j + 1) % per) * width, 1)
            r, l = carry[i]
            done.append((jnp.where(at_right, t, r), jnp.where(at_left, t, l)))
        return tuple(done)

    zero = jnp.zeros((rows, lanes), jnp.float32)
    packed = loop(per, pack, tuple((zero, zero) for _ in range(4 * groups)), 2)
    for i, (r, l) in enumerate(packed):
        to_right[i] = r
        to_left[i] = l

    lefts_there = (gy + ny_parts - 1) // ny_parts
    rights_there = (2 * ny_parts - 2 - gy) // ny_parts
    pl.semaphore_wait(barrier, 2 + 2 * lefts_there + 2 * rights_there)

    def remote(src, dst, send, recv, device):
        return pltpu.make_async_remote_copy(
            src_ref=src, dst_ref=dst, send_sem=send, recv_sem=recv,
            device_id=device, device_id_type=pl.DeviceIdType.MESH,
        )

    lefts = [
        remote(to_left, from_right.at[t], ys_sem.at[t], yr_sem.at[t], left[t]) for t in range(2)
    ]
    rights = [
        remote(to_right, from_left.at[t], ys_sem.at[2 + t], yr_sem.at[2 + t], right[t])
        for t in range(2)
    ]

    @pl.when(has_left)
    def _():
        for c in lefts:
            c.start()

    @pl.when(has_right)
    def _():
        for c in rights:
            c.start()

    xs = [
        remote(
            e.at[:, own_r, own_c], e.at[:, other_r, own_c], xs_sem.at[a], xr_sem.at[a], x_peer
        )
        for a, e in enumerate(exts)
    ]
    for a in (2, 0, 1, 3):
        xs[a].start()

    def layer(k):
        return k + gz * (n - 1 - 2 * k)

    def shift(h):
        return table[index[h]]

    def inverse(h, shape):
        return 1.0 / jnp.full(shape, shift(h), jnp.float32)

    def factor(r_at, c_at, hs, unroll):
        shape = (r_at.size, lanes)
        inv = inverse_all(hs, shape)
        one = jnp.ones(shape, jnp.float32)

        def body(k, carry):
            z = layer(k)
            rl = 1.0 / lc_x[z, r_at, c_at]
            done = []
            for (p, d), h, i in zip(carry, hs, inv):
                d = d + (rl * i) * p
                q = p + d
                p_s[h, z, r_at, c_at] = p
                pr_s[h, z, r_at, c_at] = p * rl
                b_s[h, z, r_at, c_at] = 1.0 / (p * q)
                done.append((q, d))
            return tuple(done)

        final = loop(n, body, tuple((one, one) for _ in hs), unroll)
        for (q, d), h in zip(final, hs):
            iq = 1.0 / q
            iq_s[h, r_at, c_at] = iq
            beta_s[h, r_at, c_at] = d * iq

    def inverse_all(hs, shape):
        return [inverse(h, shape) for h in hs]

    steps = list(range(half))
    factor(own_r, own_c, steps, 2)
    for a in (2, 0, 1, 3):
        xs[a].wait()
    factor(other_r, own_c, steps[:-1], 2)

    def send_beta(h, c_at, i):
        return remote(
            beta_s.at[h, :, c_at], beta_r.at[h, :, c_at], bs_sem.at[i], br_sem.at[i], z_peer
        )

    last = half - 1
    betas = [[send_beta(h, own_c, h)] for h in steps[:-1]]
    betas.append(
        [remote(
            beta_s.at[last, own_r, own_c], beta_r.at[last, own_r, own_c],
            bs_sem.at[last], br_sem.at[last], z_peer,
        )]
    )
    for b in betas:
        b[0].start()

    @pl.when(has_left)
    def _():
        for c in lefts:
            c.wait_send()
        for c in rights:
            c.wait_recv()

    @pl.when(has_right)
    def _():
        for c in rights:
            c.wait_send()
        for c in lefts:
            c.wait_recv()

    inside = ((lane < width) & has_right) | ((lane >= lanes - width) & has_left)

    def unpack(j, carry):
        at_left = slot((j + 1) % per)
        back = ((per - 1 - j) % per) * width
        for t in range(2):
            r_at = pl.ds(t * rows, rows)
            for a, e in enumerate(exts):
                for g in range(groups):
                    i = a * groups + g
                    both = jnp.where(at_left, from_right[t, i], from_left[t, i])
                    z = g * per + j
                    rest = lc_x[z, r_at, own_c] if a == 2 else jnp.zeros((rows, lanes), jnp.float32)
                    e[z, r_at, halo_c] = jnp.where(inside, pltpu.roll(both, back, 1), rest)
        return carry

    loop(per, unpack, 0, 1)

    def factor_halo(h):
        factor(all_r, halo_c, [h], 2)
        c = send_beta(h, halo_c, half + h)
        c.start()
        betas[h].append(c)

    factor_halo(0)

    wide = (2 * rows, 2 * lanes)
    row = lax.broadcasted_iota(jnp.int32, wide, 0)
    top = row == gx * rows
    bottom = row == (2 * rows - 1 + gx * rows) % (2 * rows)

    for h in steps:
        final = h == last
        r_at, c_at = (own_r, own_c) if final else (all_r, pl.ds(0, 2 * lanes))
        cut = (lambda a: a[:rows, :lanes]) if final else (lambda a: a)
        shape = (rows, lanes) if final else wide
        inv = inverse(h, shape)

        def ahead(k, total, h=h, inv=inv, cut=cut, r_at=r_at, c_at=c_at):
            z = layer(k)
            u = u_x[z]
            beside = (
                jnp.where(top, 0.0, pltpu.roll(u, 1, 0))
                + jnp.where(bottom, 0.0, pltpu.roll(u, 2 * rows - 1, 0))
                + pltpu.roll(u, 1, 1)
                + pltpu.roll(u, 2 * lanes - 1, 1)
            )
            u = cut(u)
            e = u * inv + (pc_x[z, r_at, c_at] * (cut(beside) - 4.0 * u) + src_x[z, r_at, c_at])
            total = total + pr_s[h, z, r_at, c_at] * e
            f_s[z, r_at, c_at] = total
            return total

        total = loop(n, ahead, jnp.zeros(shape, jnp.float32), 4)
        iq = iq_s[h, r_at, c_at]
        face = total * iq
        face_s[h, r_at, c_at] = face
        send = remote(
            face_s.at[h, r_at, c_at], face_r.at[h, r_at, c_at], fs_sem.at[h], fr_sem.at[h], z_peer
        )
        send.start()
        if h + 1 < last:
            factor_halo(h + 1)
        for b in betas[h]:
            b.wait()
        mine, theirs = beta_s[h, r_at, c_at], beta_r[h, r_at, c_at]
        gain = iq / (mine + theirs - mine * theirs)
        partial = (1.0 - theirs) * face
        send.wait()
        v = (face_r[h, r_at, c_at] + partial) * gain

        def behind(k, v, h=h, final=final, r_at=r_at, c_at=c_at):
            z = layer(k)
            v = v + f_s[z, r_at, c_at] * b_s[h, z, r_at, c_at]
            w = p_s[h, z, r_at, c_at] * v
            if final:
                out[z] = w
            else:
                u_x[z] = w
            return v

        loop(n, behind, v, 4, reverse=True)


def solution(mesh):
    ny_parts = mesh.shape["gy"]
    assert mesh.shape["gz"] == 2 and mesh.shape["gx"] == 2

    def on_device(u, pc, lc, src, table, index):
        half = index.shape[0]
        n, rows, lanes = u.shape
        f32 = jnp.float32
        ext = pltpu.VMEM((n, 2 * rows, 2 * lanes), f32)
        coef = pltpu.VMEM((half, n, 2 * rows, 2 * lanes), f32)
        face = pltpu.VMEM((half, 2 * rows, 2 * lanes), f32)
        count = 4 * (n * half // lanes)
        pack = pltpu.VMEM((count, rows, lanes), f32)
        packs = pltpu.VMEM((2, count, rows, lanes), f32)
        dma = pltpu.SemaphoreType.DMA
        return pl.pallas_call(
            functools.partial(kernel, ny_parts, half),
            out_shape=jax.ShapeDtypeStruct(u.shape, f32),
            in_specs=[pl.BlockSpec(memory_space=pl.ANY)] * 4
            + [pl.BlockSpec(memory_space=pltpu.SMEM)] * 2,
            out_specs=pl.BlockSpec(memory_space=pltpu.VMEM),
            scratch_shapes=[ext] * 4 + [pack] * 2 + [packs] * 2
            + [coef] * 3 + [ext] + [face] * 5
            + [dma((4,)), dma((4,)), dma((4,)), dma((4,)), dma((4,)),
               dma((2 * half,)), dma((2 * half,)), dma((half,)), dma((half,))],
            compiler_params=pltpu.CompilerParams(collective_id=0, has_side_effects=True),
        )(u, pc, lc, src, table, index)

    spec = P("gz", "gx", "gy")
    return jax.shard_map(
        on_device, mesh=mesh, in_specs=(spec,) * 4 + (P(), P()), out_specs=spec, check_vma=False
    )
```

time: 318 us -> 33.4 us (0.11); the launches traced: 313 us -> 33.3 us
  blocking collectives: 104 us -> 0 us
  waiting for transfers between devices: 81.5 us -> 0 us
  local copies, waits for them, and re-layouts: 46.7 us -> 1.67 us
  starting transfers between devices: 42.7 us -> 0 us
  other arithmetic: 34.9 us -> 0 us
  Pallas kernels: 0 us -> 31.6 us
    all_gather x24 -> x0, blocking collectives: 104 us -> none  [the longest x4 17.4 us: reduced_gathered(): lax.all_gather(last_y[None], 'gz', axis=0, tiled=True)]
    ppermute x16 -> x0, waiting for transfers between devices: 81.5 us -> none  [the longest x8 81.5 us: padded_2(): lax.ppermute(tail, axis, [(i, (i + 1) % count) for i in range(ends)])]
    ppermute x16 -> x0, starting transfers between devices: 42.7 us -> none  [the longest x8 31.8 us: padded_2(): lax.ppermute(tail, axis, [(i, (i + 1) % count) for i in range(ends)])]
    unnamed x202 -> x1, local copies, waits for them, and re-layouts: 33.8 us -> 1.67 us
    pallas_call x0 -> x1, Pallas kernels: none -> 31.6 us  [on_device(): pl.pallas_call(functools.partial(kernel, ny_parts, half), out_shape=jax.S...]
    add x54 -> x0, other arithmetic: 16.7 us -> none  [the longest x22 12.5 us: local_solve(): main_band + left_factor * upper_before + right_factor * lower_after]
    slice x104 -> x0, local copies, waits for them, and re-layouts: 12.8 us -> none  [the longest x60 4.68 us: from_below(): lax.slice_in_dim(values, 0, values.shape[which_axis] - stride, axis=which...]
    another operation x8 -> x0, other arithmetic: 8.82 us -> none  [on_device(): jnp.stack([explicit, jnp.where(layer_index == 0, scaled, zero_field), jnp...]
  transfers between devices with their start and end apart: 16 -> 0, of which waited for: 5 -> 0; matrix products, arithmetic and copies ran while one was open for 8% -> 0% of each run, Pallas kernels for 0% -> 0%
where the time goes in v1:
time: 33.4 us; the launch traced here: 33.3 us
  Pallas kernels  31.6 us (95%)
  local copies, waits for them, and re-layouts  1.67 us (5%)
    pallas_call x1, Pallas kernels, on_device(): pl.pallas_call(functools.partial(kernel, ny_parts, half), out_shape=jax.S...  31.6 us
    unnamed x1, local copies, waits for them, and re-layouts  1.67 us

profile of v1, /device:TPU:0, one launch (start us, length us, event | category | flops | bytes accessed | tf_op | source)
XLA Modules:
  0.0 33.3 jit_solution(5914454482085489021)
XLA Ops:
  0.0 31.6 %shard_map.64 = f32[64,8,128]{2,1,0:T(8,128)} custom-call(f32[64,8,128]{2,1,0:T(8,128)} %u_in.1, f32[64,8,128]{2,1,0:T(8,128)} %pc_in.1, f32[64,8,128]{2,1,0:T(8,128)} %lc_in.1, f32[64,8,128]{2,1,0:T(8,128)} %src_in.1, f32[8]{0:T(128)} %table.1, s32[4]{0:T(128)} %index.1), custom_call_target="tpu_custom_call" | custom-call | tf_op jit(solution)/shard_map/pallas_call | solution.py:307
  31.6 1.7 %copy.8 = f32[64,8,128]{2,1,0:T(8,128)} copy(f32[64,8,128]{2,1,0:T(8,128)} %shard_map.64) | data formatting | bytes 524288

commit v2 on v1

--- a/solution.py
+++ b/solution.py
@@ -6,6 +6,13 @@
 from jax.experimental import pallas as pl
 from jax.experimental.pallas import tpu as pltpu
 from jax.sharding import PartitionSpec as P
+
+
+EXPLICIT = 16
+SUMS = 8
+PACK = 4
+UNPACK = 4
+FACTOR = 2
 
 
 def loop(count, body, init, unroll, reverse=False):
@@ -91,7 +98,7 @@
         return tuple(done)
 
     zero = jnp.zeros((rows, lanes), jnp.float32)
-    packed = loop(per, pack, tuple((zero, zero) for _ in range(4 * groups)), 2)
+    packed = loop(per, pack, tuple((zero, zero) for _ in range(4 * groups)), PACK)
     for i, (r, l) in enumerate(packed):
         to_right[i] = r
         to_left[i] = l
@@ -142,7 +149,7 @@
     def inverse(h, shape):
         return 1.0 / jnp.full(shape, shift(h), jnp.float32)
 
-    def factor(r_at, c_at, hs, unroll):
+    def factor(r_at, c_at, hs):
         shape = (r_at.size, lanes)
         inv = inverse_all(hs, shape)
         one = jnp.ones(shape, jnp.float32)
@@ -160,7 +167,7 @@
                 done.append((q, d))
             return tuple(done)
 
-        final = loop(n, body, tuple((one, one) for _ in hs), unroll)
+        final = loop(n, body, tuple((one, one) for _ in hs), FACTOR)
         for (q, d), h in zip(final, hs):
             iq = 1.0 / q
             iq_s[h, r_at, c_at] = iq
@@ -170,10 +177,10 @@
         return [inverse(h, shape) for h in hs]
 
     steps = list(range(half))
-    factor(own_r, own_c, steps, 2)
+    factor(own_r, own_c, steps)
     for a in (2, 0, 1, 3):
         xs[a].wait()
-    factor(other_r, own_c, steps[:-1], 2)
+    factor(other_r, own_c, steps[:-1])
 
     def send_beta(h, c_at, i):
         return remote(
@@ -221,10 +228,10 @@
                     e[z, r_at, halo_c] = jnp.where(inside, pltpu.roll(both, back, 1), rest)
         return carry
 
-    loop(per, unpack, 0, 1)
+    loop(per, unpack, 0, UNPACK)
 
     def factor_halo(h):
-        factor(all_r, halo_c, [h], 2)
+        factor(all_r, halo_c, [h])
         c = send_beta(h, halo_c, half + h)
         c.start()
         betas[h].append(c)
@@ -236,29 +243,38 @@
     top = row == gx * rows
     bottom = row == (2 * rows - 1 + gx * rows) % (2 * rows)
 
+    def edges(u):
+        return (
+            jnp.where(top, 0.0, pltpu.roll(u, 1, 0))
+            + jnp.where(bottom, 0.0, pltpu.roll(u, 2 * rows - 1, 0))
+            + pltpu.roll(u, 1, 1)
+            + pltpu.roll(u, 2 * lanes - 1, 1)
+        )
+
+    def explicit(h, field):
+        r_at, c_at, shape, cut = part(h)
+        inv = inverse(h, shape)
+
+        def body(k, total):
+            z = layer(k)
+            u = field(z)
+            beside = cut(edges(u))
+            u = cut(u)
+            e = u * inv + (pc_x[z, r_at, c_at] * (beside - 4.0 * u) + src_x[z, r_at, c_at])
+            g = pr_s[h, z, r_at, c_at] * e
+            f_s[z, r_at, c_at] = g
+            return total + g
+
+        return loop(n, body, jnp.zeros(shape, jnp.float32), EXPLICIT)
+
+    def part(h):
+        if h == last:
+            return own_r, own_c, (rows, lanes), lambda a: a[:rows, :lanes]
+        return all_r, pl.ds(0, 2 * lanes), wide, lambda a: a
+
+    total = explicit(0, lambda z: u_x[z])
     for h in steps:
-        final = h == last
-        r_at, c_at = (own_r, own_c) if final else (all_r, pl.ds(0, 2 * lanes))
-        cut = (lambda a: a[:rows, :lanes]) if final else (lambda a: a)
-        shape = (rows, lanes) if final else wide
-        inv = inverse(h, shape)
-
-        def ahead(k, total, h=h, inv=inv, cut=cut, r_at=r_at, c_at=c_at):
-            z = layer(k)
-            u = u_x[z]
-            beside = (
-                jnp.where(top, 0.0, pltpu.roll(u, 1, 0))
-                + jnp.where(bottom, 0.0, pltpu.roll(u, 2 * rows - 1, 0))
-                + pltpu.roll(u, 1, 1)
-                + pltpu.roll(u, 2 * lanes - 1, 1)
-            )
-            u = cut(u)
-            e = u * inv + (pc_x[z, r_at, c_at] * (cut(beside) - 4.0 * u) + src_x[z, r_at, c_at])
-            total = total + pr_s[h, z, r_at, c_at] * e
-            f_s[z, r_at, c_at] = total
-            return total
-
-        total = loop(n, ahead, jnp.zeros(shape, jnp.float32), 4)
+        r_at, c_at, shape, _ = part(h)
         iq = iq_s[h, r_at, c_at]
         face = total * iq
         face_s[h, r_at, c_at] = face
@@ -266,6 +282,22 @@
             face_s.at[h, r_at, c_at], face_r.at[h, r_at, c_at], fs_sem.at[h], fr_sem.at[h], z_peer
         )
         send.start()
+        zero_part = jnp.zeros(shape, jnp.float32)
+
+        def ahead(k, total, h=h, r_at=r_at, c_at=c_at):
+            z = layer(k)
+            total = total + f_s[z, r_at, c_at]
+            f_s[z, r_at, c_at] = total * b_s[h, z, r_at, c_at]
+            return total
+
+        def behind(k, total, h=h, r_at=r_at, c_at=c_at):
+            z = layer(k)
+            total = total + f_s[z, r_at, c_at]
+            f_s[z, r_at, c_at] = p_s[h, z, r_at, c_at] * total
+            return total
+
+        loop(n, ahead, zero_part, SUMS)
+        loop(n, behind, zero_part, SUMS, reverse=True)
         if h + 1 < last:
             factor_halo(h + 1)
         for b in betas[h]:
@@ -276,17 +308,18 @@
         send.wait()
         v = (face_r[h, r_at, c_at] + partial) * gain
 
-        def behind(k, v, h=h, final=final, r_at=r_at, c_at=c_at):
-            z = layer(k)
-            v = v + f_s[z, r_at, c_at] * b_s[h, z, r_at, c_at]
-            w = p_s[h, z, r_at, c_at] * v
-            if final:
-                out[z] = w
-            else:
-                u_x[z] = w
-            return v
-
-        loop(n, behind, v, 4, reverse=True)
+        def solved(z, h=h, v=v, r_at=r_at, c_at=c_at):
+            return p_s[h, z, r_at, c_at] * v + f_s[z, r_at, c_at]
+
+        if h < last:
+            total = explicit(h + 1, solved)
+        else:
+
+            def write(z, carry):
+                out[z] = solved(z)
+                return carry
+
+            loop(n, write, 0, SUMS)
 
 
 def solution(mesh):

time: 33.4 us -> 39.9 us (1.19)
  Pallas kernels: 31.6 us -> 38.1 us
    pallas_call x1, Pallas kernels: 31.6 us -> 38.1 us  [on_device(): pl.pallas_call(functools.partial(kernel, ny_parts, half), out_shape=jax.S...]
where the time goes in v2:
time: 39.9 us; the launch traced here: 39.8 us
  Pallas kernels  38.1 us (95%)
  local copies, waits for them, and re-layouts  1.67 us (4%)
    pallas_call x1, Pallas kernels, on_device(): pl.pallas_call(functools.partial(kernel, ny_parts, half), out_shape=jax.S...  38.1 us
    unnamed x1, local copies, waits for them, and re-layouts  1.67 us

profile of v2, /device:TPU:0, one launch (start us, length us, event | category | flops | bytes accessed | tf_op | source)
XLA Modules:
  0.0 39.8 jit_solution(15754472901051669008)
XLA Ops:
  0.0 38.1 %shard_map.64 = f32[64,8,128]{2,1,0:T(8,128)} custom-call(f32[64,8,128]{2,1,0:T(8,128)} %u_in.1, f32[64,8,128]{2,1,0:T(8,128)} %pc_in.1, f32[64,8,128]{2,1,0:T(8,128)} %lc_in.1, f32[64,8,128]{2,1,0:T(8,128)} %src_in.1, f32[8]{0:T(128)} %table.1, s32[4]{0:T(128)} %index.1), custom_call_target="tpu_custom_call" | custom-call | tf_op jit(solution)/shard_map/pallas_call | solution.py:340
  38.1 1.7 %copy.8 = f32[64,8,128]{2,1,0:T(8,128)} copy(f32[64,8,128]{2,1,0:T(8,128)} %shard_map.64) | data formatting | bytes 524288

commit v3 on v2

--- a/solution.py
+++ b/solution.py
@@ -33,7 +33,7 @@
     u_in, pc_in, lc_in, src_in, table, index,
     out,
     u_x, pc_x, lc_x, src_x, to_left, to_right, from_left, from_right,
-    p_s, pr_s, b_s, f_s, iq_s, beta_s, beta_r, face_s, face_r,
+    p_s, pr_s, b_s, g_s, f_s, w_s, iq_s, beta_s, beta_r, face_s, face_r,
     in_sem, xs_sem, xr_sem, ys_sem, yr_sem, bs_sem, br_sem, fs_sem, fr_sem,
 ):
     n, rows, lanes = u_in.shape
@@ -89,10 +89,10 @@
 
     def pack(j, carry):
         at_right = slot(j)
-        at_left = slot((j + 1) % per)
+        at_left = slot(lax.rem(j + 1, per))
         done = []
         for i, (e, g) in enumerate((e, g) for e in exts for g in range(groups)):
-            t = pltpu.roll(e[g * per + j, own_r, own_c], ((j + 1) % per) * width, 1)
+            t = pltpu.roll(e[g * per + j, own_r, own_c], (lax.rem(j + 1, per)) * width, 1)
             r, l = carry[i]
             done.append((jnp.where(at_right, t, r), jnp.where(at_left, t, l)))
         return tuple(done)
@@ -214,9 +214,11 @@
 
     inside = ((lane < width) & has_right) | ((lane >= lanes - width) & has_left)
 
+    filler = lc_x[0, own_r, own_c]
+
     def unpack(j, carry):
-        at_left = slot((j + 1) % per)
-        back = ((per - 1 - j) % per) * width
+        at_left = slot(lax.rem(j + 1, per))
+        back = (per - 1 - j) * width
         for t in range(2):
             r_at = pl.ds(t * rows, rows)
             for a, e in enumerate(exts):
@@ -224,7 +226,7 @@
                     i = a * groups + g
                     both = jnp.where(at_left, from_right[t, i], from_left[t, i])
                     z = g * per + j
-                    rest = lc_x[z, r_at, own_c] if a == 2 else jnp.zeros((rows, lanes), jnp.float32)
+                    rest = filler if a == 2 else zero
                     e[z, r_at, halo_c] = jnp.where(inside, pltpu.roll(both, back, 1), rest)
         return carry
 
@@ -262,7 +264,7 @@
             u = cut(u)
             e = u * inv + (pc_x[z, r_at, c_at] * (beside - 4.0 * u) + src_x[z, r_at, c_at])
             g = pr_s[h, z, r_at, c_at] * e
-            f_s[z, r_at, c_at] = g
+            g_s[z, r_at, c_at] = g
             return total + g
 
         return loop(n, body, jnp.zeros(shape, jnp.float32), EXPLICIT)
@@ -286,14 +288,14 @@
 
         def ahead(k, total, h=h, r_at=r_at, c_at=c_at):
             z = layer(k)
-            total = total + f_s[z, r_at, c_at]
+            total = total + g_s[z, r_at, c_at]
             f_s[z, r_at, c_at] = total * b_s[h, z, r_at, c_at]
             return total
 
         def behind(k, total, h=h, r_at=r_at, c_at=c_at):
             z = layer(k)
             total = total + f_s[z, r_at, c_at]
-            f_s[z, r_at, c_at] = p_s[h, z, r_at, c_at] * total
+            w_s[z, r_at, c_at] = p_s[h, z, r_at, c_at] * total
             return total
 
         loop(n, ahead, zero_part, SUMS)
@@ -309,7 +311,7 @@
         v = (face_r[h, r_at, c_at] + partial) * gain
 
         def solved(z, h=h, v=v, r_at=r_at, c_at=c_at):
-            return p_s[h, z, r_at, c_at] * v + f_s[z, r_at, c_at]
+            return p_s[h, z, r_at, c_at] * v + w_s[z, r_at, c_at]
 
         if h < last:
             total = explicit(h + 1, solved)
@@ -344,7 +346,7 @@
             + [pl.BlockSpec(memory_space=pltpu.SMEM)] * 2,
             out_specs=pl.BlockSpec(memory_space=pltpu.VMEM),
             scratch_shapes=[ext] * 4 + [pack] * 2 + [packs] * 2
-            + [coef] * 3 + [ext] + [face] * 5
+            + [coef] * 3 + [ext] * 3 + [face] * 5
             + [dma((4,)), dma((4,)), dma((4,)), dma((4,)), dma((4,)),
                dma((2 * half,)), dma((2 * half,)), dma((half,)), dma((half,))],
             compiler_params=pltpu.CompilerParams(collective_id=0, has_side_effects=True),

time: 39.9 us -> 26.6 us (0.67)
  Pallas kernels: 38.1 us -> 24.7 us
    pallas_call x1, Pallas kernels: 38.1 us -> 24.7 us  [on_device(): pl.pallas_call(functools.partial(kernel, ny_parts, half), out_shape=jax.S...]
where the time goes in v3:
time: 26.6 us; the launch traced here: 26.4 us
  Pallas kernels  24.7 us (93%)
  local copies, waits for them, and re-layouts  1.67 us (6%)
    pallas_call x1, Pallas kernels, on_device(): pl.pallas_call(functools.partial(kernel, ny_parts, half), out_shape=jax.S...  24.7 us
    unnamed x1, local copies, waits for them, and re-layouts  1.67 us

profile of v3, /device:TPU:0, one launch (start us, length us, event | category | flops | bytes accessed | tf_op | source)
XLA Modules:
  0.0 26.4 jit_solution(17593610542099846239)
XLA Ops:
  0.0 24.7 %shard_map.64 = f32[64,8,128]{2,1,0:T(8,128)} custom-call(f32[64,8,128]{2,1,0:T(8,128)} %u_in.1, f32[64,8,128]{2,1,0:T(8,128)} %pc_in.1, f32[64,8,128]{2,1,0:T(8,128)} %lc_in.1, f32[64,8,128]{2,1,0:T(8,128)} %src_in.1, f32[8]{0:T(128)} %table.1, s32[4]{0:T(128)} %index.1), custom_call_target="tpu_custom_call" | custom-call | tf_op jit(solution)/shard_map/pallas_call | solution.py:342
  24.7 1.7 %copy.8 = f32[64,8,128]{2,1,0:T(8,128)} copy(f32[64,8,128]{2,1,0:T(8,128)} %shard_map.64) | data formatting | bytes 524288

commit v4 on v3

--- a/solution.py
+++ b/solution.py
@@ -8,11 +8,11 @@
 from jax.sharding import PartitionSpec as P
 
 
-EXPLICIT = 16
+EXPLICIT = 32
 SUMS = 8
-PACK = 4
-UNPACK = 4
-FACTOR = 2
+PACK = 16
+UNPACK = 16
+FACTOR = 8
 
 
 def loop(count, body, init, unroll, reverse=False):
@@ -33,7 +33,7 @@
     u_in, pc_in, lc_in, src_in, table, index,
     out,
     u_x, pc_x, lc_x, src_x, to_left, to_right, from_left, from_right,
-    p_s, pr_s, b_s, g_s, f_s, w_s, iq_s, beta_s, beta_r, face_s, face_r,
+    p_s, own_s, near_s, src_s, b_s, g_s, f_s, w_s, iq_s, beta_s, beta_r, face_s, face_r,
     in_sem, xs_sem, xr_sem, ys_sem, yr_sem, bs_sem, br_sem, fs_sem, fr_sem,
 ):
     n, rows, lanes = u_in.shape
@@ -157,12 +157,17 @@
         def body(k, carry):
             z = layer(k)
             rl = 1.0 / lc_x[z, r_at, c_at]
+            pc, src = pc_x[z, r_at, c_at], src_x[z, r_at, c_at]
+            four = 4.0 * pc
             done = []
             for (p, d), h, i in zip(carry, hs, inv):
                 d = d + (rl * i) * p
                 q = p + d
                 p_s[h, z, r_at, c_at] = p
-                pr_s[h, z, r_at, c_at] = p * rl
+                pr = p * rl
+                own_s[h, z, r_at, c_at] = pr * (i - four)
+                near_s[h, z, r_at, c_at] = pr * pc
+                src_s[h, z, r_at, c_at] = pr * src
                 b_s[h, z, r_at, c_at] = 1.0 / (p * q)
                 done.append((q, d))
             return tuple(done)
@@ -255,15 +260,14 @@
 
     def explicit(h, field):
         r_at, c_at, shape, cut = part(h)
-        inv = inverse(h, shape)
 
         def body(k, total):
             z = layer(k)
             u = field(z)
             beside = cut(edges(u))
-            u = cut(u)
-            e = u * inv + (pc_x[z, r_at, c_at] * (beside - 4.0 * u) + src_x[z, r_at, c_at])
-            g = pr_s[h, z, r_at, c_at] * e
+            g = own_s[h, z, r_at, c_at] * cut(u) + (
+                near_s[h, z, r_at, c_at] * beside + src_s[h, z, r_at, c_at]
+            )
             g_s[z, r_at, c_at] = g
             return total + g
 
@@ -341,12 +345,12 @@
         dma = pltpu.SemaphoreType.DMA
         return pl.pallas_call(
             functools.partial(kernel, ny_parts, half),
-            out_shape=jax.ShapeDtypeStruct(u.shape, f32),
+            out_shape=pltpu.VMEM(u.shape, f32),
             in_specs=[pl.BlockSpec(memory_space=pl.ANY)] * 4
             + [pl.BlockSpec(memory_space=pltpu.SMEM)] * 2,
             out_specs=pl.BlockSpec(memory_space=pltpu.VMEM),
             scratch_shapes=[ext] * 4 + [pack] * 2 + [packs] * 2
-            + [coef] * 3 + [ext] * 3 + [face] * 5
+            + [coef] * 5 + [ext] * 3 + [face] * 5
             + [dma((4,)), dma((4,)), dma((4,)), dma((4,)), dma((4,)),
                dma((2 * half,)), dma((2 * half,)), dma((half,)), dma((half,))],
             compiler_params=pltpu.CompilerParams(collective_id=0, has_side_effects=True),

time: 26.6 us -> 23.1 us (0.87)
  Pallas kernels: 24.7 us -> 22.2 us
  local copies, waits for them, and re-layouts: 1.67 us -> 0.71 us
    pallas_call x1, Pallas kernels: 24.7 us -> 22.2 us  [on_device(): pl.pallas_call(functools.partial(kernel, ny_parts, half), out_shape=pltpu...]
    unnamed x1, local copies, waits for them, and re-layouts: 1.67 us -> 0.71 us
where the time goes in v4:
time: 23.1 us; the launch traced here: 22.9 us
  Pallas kernels  22.2 us (96%)
  local copies, waits for them, and re-layouts  0.71 us (3%)
    pallas_call x1, Pallas kernels, on_device(): pl.pallas_call(functools.partial(kernel, ny_parts, half), out_shape=pltpu...  22.2 us
    unnamed x1, local copies, waits for them, and re-layouts  0.71 us

profile of v4, /device:TPU:0, one launch (start us, length us, event | category | flops | bytes accessed | tf_op | source)
XLA Modules:
  0.0 22.9 jit_solution(11152385516510266066)
XLA Ops:
  0.0 22.2 %shard_map.64 = f32[64,8,128]{2,1,0:T(8,128)S(1)} custom-call(f32[64,8,128]{2,1,0:T(8,128)} %u_in.1, f32[64,8,128]{2,1,0:T(8,128)} %pc_in.1, f32[64,8,128]{2,1,0:T(8,128)} %lc_in.1, f32[64,8,128]{2,1,0:T(8,128)} %src_in.1, f32[8]{0:T(128)} %table.1, s32[4]{0:T(128)} %index.1), custom_call_target="tpu_custom_call" | custom-call | tf_op jit(solution)/shard_map/pallas_call | solution.py:346
  22.2 0.7 %copy.8 = f32[64,8,128]{2,1,0:T(8,128)} copy(f32[64,8,128]{2,1,0:T(8,128)S(1)} %shard_map.64) | data formatting | bytes 524288
